TPU v7x, 32 devices: a whole 2x2x4 slice. The times are simulated.
32 devices in a mesh: band: 8 (over z, x), ga: 4 (over y, core).
Axes of the slice: x: 2, y: 2, z: 4, core: 2. Of those that a mesh axis runs over, the one named last changes fastest.
Arguments:
- elements: bfloat16 [2, 768, 2048], P(None, 'band', 'ga'), may hold values from -0.75 to 0.75
- screened: bfloat16 [2, 2, 2048, 2048], P(None, None, 'ga'), may hold values from -0.09375 to 0.09375
- energies: float32 [768], replicated, may hold values from -3 to 3
- freq_points: float32 [2], replicated, may hold values from -3 to 3
- freq_weights: float32 [2], replicated, may hold values from 0.5 to 2
- band_of_slot: int32 [768], replicated, may hold values from 0 to 767, each once
Outputs:
- sigma: float32 [2, 768, 768], P(None, 'band', 'ga')
Inputs may be any that keep to these rules, and one draw needn't show every extreme that they name: `band_of_slot`: each of 0 to 767 stands once.
All inputs are finite; a program needn't handle non-finite values.
Results may differ from a plain program's by a relative error of at most 0.0042.
Values may be sent and summed in bfloat16 or wider, within the bound.
A program may use at most 128 MiB of HBM per device.

v0:
```python
import functools

import jax
import jax.numpy as jnp
from jax import lax
from jax.experimental import pallas as pl
from jax.experimental.pallas import tpu as pltpu
from jax.sharding import PartitionSpec as P

MESH = pl.DeviceIdType.MESH
F32 = jnp.float32
BF16 = jnp.bfloat16
NT = (((1,), (1,)), ((), ()))


def kernel(nb, ng, nx, el, wh, en_h, bos_h, fp_h, fw_h, out, *scratch):
    (en, bos, fp, fw, in_sem, gat, wv, a_ref, e3, scr, held, dsend, drecv, ysend, yrecv, lv, ssend, srecv, own,
     loc_sem, w_sem, up_sem, dn_sem, x_sem, g_recv, d_ss, d_rs, y_ss, y_rs, s_ss, s_rs) = scratch
    rows, depth = el.shape[1], el.shape[2]
    quarter = wh.shape[3] // ng
    nz, ny = nb // nx, ng // 2
    per = nb // ng
    slots = en.shape[0]
    b, g = lax.axis_index("band"), lax.axis_index("ga")
    z, x = b // nx, lax.rem(b, nx)
    y, c = g // 2, lax.rem(g, 2)
    mate = g + 1 - 2 * c
    xb = z * nx + (nx - 1 - x)

    barrier = pltpu.get_barrier_semaphore()

    def greet(band, ga):
        pl.semaphore_signal(barrier, inc=1, device_id=(band, ga), device_id_type=MESH)

    greet(xb, g)

    @pl.when(z > 0)
    def _():
        greet(b - nx, g)

    @pl.when(z < nz - 1)
    def _():
        greet(b + nx, g)

    for r in range(1, ng):
        greet(b, lax.rem(g + r, ng))

    small = [pltpu.make_async_copy(s, t, in_sem.at[i]) for i, (s, t) in enumerate(
        ((en_h, en), (bos_h, bos), (fp_h, fp), (fw_h, fw)))]
    mine = gat.at[:, pl.ds(pl.multiple_of(b * rows, rows), rows), :]
    local = pltpu.make_async_copy(el, mine, loc_sem)
    local.start()
    for copy in small:
        copy.start()

    def q_of(other, d):
        core = (1 - c) if other else c
        return lax.rem(y + d, ny) * 2 + core

    order = []
    for d in list(range(1, ny)) + [0]:
        order += [(1, d), (0, d)]

    def w_copy(k, w):
        o, d = order[k]
        cols = pl.ds(pl.multiple_of(q_of(o, d) * quarter, quarter), quarter)
        return pltpu.make_async_copy(wh.at[w, :, :, cols], wv.at[w, k], w_sem.at[w, k])

    below = jnp.where(z > 0, 1, 0)
    above = jnp.where(z < nz - 1, 1, 0)
    local.wait()
    for k in range(ng):
        for w in range(2):
            w_copy(k, w).start()
    pl.semaphore_wait(barrier, ng + below + above)

    unit = rows // 6
    pieces = ((0, 2 * unit), (2 * unit, 2 * unit), (4 * unit, unit), (5 * unit, unit))
    last = len(pieces) - 1

    def send(src, i, dst, sem):
        start, size = pieces[i]
        ref = gat.at[:, pl.ds(pl.multiple_of(src * rows + start, unit), size), :]
        return pltpu.make_async_remote_copy(
            src_ref=ref, dst_ref=ref, send_sem=sem, recv_sem=g_recv.at[src, i],
            device_id=(dst, g), device_id_type=MESH)

    def arrived(src, i):
        send(src, i, xb, x_sem.at[0, i]).wait_recv()

    def send_z(src, i, up, down):
        if up:
            @pl.when(z < nz - 1)
            def _():
                send(src, i, b + nx, up_sem.at[src, i]).start()

        if down:
            @pl.when(z > 0)
            def _():
                send(src, i, b - nx, dn_sem.at[src, i]).start()

    def fwd(s, only=None):
        for i in range(last) if only is None else (only,):
            for zs, up in ((z - s, True), (z + s, False)):
                @pl.when((zs >= 0) & (zs < nz))
                def _():
                    src = zs * nx + x
                    arrived(src, i)
                    send_z(src, i, up, not up)
                    send(src, i, xb, x_sem.at[zs, i]).start()

    def fwd_last(s):
        for zs, up in ((z - s, True), (z + s, False)):
            @pl.when((zs >= 0) & (zs < nz))
            def _():
                for v in (x, nx - 1 - x):
                    arrived(zs * nx + v, last)
                    send_z(zs * nx + v, last, up, not up)

    send(b, last, xb, x_sem.at[z, last]).start()
    for i in range(last + 1):
        send_z(b, i, True, True)
        if i < last:
            send(b, i, xb, x_sem.at[z, i]).start()

    for copy in small:
        copy.wait()
    row = lax.broadcasted_iota(jnp.int32, (16, slots), 0)
    e = en[...].reshape(1, slots)
    hi = e.astype(BF16).astype(F32)
    mid = (e - hi).astype(BF16).astype(F32)
    lo = e - hi - mid
    e3[...] = jnp.where(row == 0, hi, jnp.where(row == 1, mid, jnp.where(row == 2, lo, 0.0))).astype(BF16)
    tile = slots if slots <= 1024 else 8 * rows

    for u in range(slots // tile):
        slot = bos[u * tile : (u + 1) * tile].reshape(1, tile)

        def add(j, acc):
            at = pl.multiple_of(j * tile, tile)
            hit = lax.broadcasted_iota(jnp.int32, (tile, tile), 0) + at == slot
            return acc + jnp.dot(e3[:, pl.ds(at, tile)], jnp.where(hit, 1.0, 0.0).astype(BF16),
                                 preferred_element_type=F32)

        acc = lax.fori_loop(0, slots // tile, add, jnp.zeros((16, tile), F32))
        energy = jnp.sum(acc, axis=0, keepdims=True)
        for w in range(2):
            off = energy - fp[w]
            value = 0.5 * (fw[w] / (1.0 + 4.0 * off * off))
            for v in range(tile // rows):
                scr[u * (tile // rows) + v, w : w + 1, :] = value[:, v * rows : (v + 1) * rows]
    pick = lax.broadcasted_iota(jnp.int32, (rows, rows), 1) == lax.broadcasted_iota(
        jnp.int32, (rows, rows), 0)
    cols = [jnp.sum(jnp.where(pick, scr[b, w : w + 1, :], 0.0), axis=1, keepdims=True)
            for w in range(2)]

    er = gat[0, pl.ds(pl.multiple_of(b * rows, rows), rows), :]
    ei = gat[1, pl.ds(pl.multiple_of(b * rows, rows), rows), :]
    a_ref[:rows, :depth] = er
    a_ref[:rows, depth:] = ei
    a_ref[rows:, :depth] = -ei
    a_ref[rows:, depth:] = er

    def d_copy(d, w):
        return pltpu.make_async_remote_copy(
            src_ref=dsend.at[d, w], dst_ref=drecv.at[d, w], send_sem=d_ss.at[d, w],
            recv_sem=d_rs.at[d, w], device_id=(b, mate), device_id_type=MESH)

    def y_copy(d, w):
        return pltpu.make_async_remote_copy(
            src_ref=ysend.at[d - 1, w], dst_ref=yrecv.at[d - 1, w], send_sem=y_ss.at[d - 1, w],
            recv_sem=y_rs.at[d - 1, w], device_id=(b, lax.rem(y + d, ny) * 2 + c),
            device_id_type=MESH)

    def pass_on(d):
        for w in range(2):
            d_copy(d, w).wait_recv()
            ysend[d - 1, w] = (held[d, w] + drecv[d, w].astype(F32)).astype(BF16)
            y_copy(d, w).start()

    for k in range(ng):
        o, d = order[k]
        for w in range(2):
            w_copy(k, w).wait()
            part = jnp.dot(a_ref[...], wv[w, k].reshape(2 * depth, quarter),
                           preferred_element_type=F32)
            if o:
                dsend[d, w] = part.astype(BF16)
                d_copy(d, w).start()
            else:
                held[d, w] = part
        if o and k >= 2:
            pass_on(order[k - 1][1])

    def consume_block(k):
        at = pl.ds(pl.multiple_of(k * rows, rows), rows)
        pr = lax.dot_general(lv[0], gat[0, at, :], NT, preferred_element_type=F32)
        pr = pr + lax.dot_general(lv[1], gat[1, at, :], NT, preferred_element_type=F32)
        f = [cols[w] + scr[k, w : w + 1, :] for w in range(2)]
        total = [f[0] * pr[i * rows : (i + 1) * rows]
                 + f[1] * pr[(2 + i) * rows : (3 + i) * rows] for i in range(2)]
        q, p = k // per, lax.rem(k, per)

        @pl.when(q == g)
        def _():
            for i in range(2):
                own[p, i] = total[i]

        @pl.when(q != g)
        def _():
            for i in range(2):
                ssend[k, i] = total[i].astype(BF16)
            slot = lax.rem(g - q + ng, ng) - 1
            pltpu.make_async_remote_copy(
                src_ref=ssend.at[k], dst_ref=srecv.at[slot, p], send_sem=s_ss.at[k],
                recv_sem=s_rs.at[slot, p], device_id=(b, q), device_id_type=MESH).start()

    def each_side(s, act):
        @pl.when(z - s >= 0)
        def _():
            act(z - s)

        if not (isinstance(s, int) and s == 0):
            @pl.when(z + s < nz)
            def _():
                act(z + s)

    def consume_own(s):
        each_side(s, lambda zs: consume_block(zs * nx + x))

    def consume_other(s):
        def act(zs):
            k = zs * nx + (nx - 1 - x)
            for i in range(last):
                arrived(k, i)
            consume_block(k)

        each_side(s, act)

    arrived(xb, last)
    send_z(xb, last, True, True)
    ahead = 3
    fwd(1)
    fwd(2)
    fwd_last(1)
    inner = (z > 0) & (z < nz - 1)

    @pl.when(inner)
    def _():
        fwd_last(2)

    fwd(ahead, 0)

    for w in range(2):
        total = held[0, w]
        d_copy(0, w).wait_recv()
        total = total + drecv[0, w].astype(F32)
        for d in range(1, ny):
            y_copy(d, w).wait_recv()
            total = total + yrecv[d - 1, w].astype(F32)
        total = total.astype(BF16)
        lv[0, 2 * w * rows : 2 * (w + 1) * rows, :] = total
        lv[1, 2 * w * rows : (2 * w + 1) * rows, :] = -total[rows:]
        lv[1, (2 * w + 1) * rows : (2 * w + 2) * rows, :] = total[:rows]

    consume_own(0)
    consume_other(0)
    consume_own(1)
    fwd(ahead, 1)
    consume_other(1)
    fwd(ahead, 2)

    @pl.when(jnp.logical_not(inner))
    def _():
        fwd_last(2)

    consume_own(2)
    consume_other(2)
    fwd_last(ahead)
    consume_own(ahead)

    def tail(s, carry):
        fwd(s)
        fwd_last(s)
        consume_own(s)
        consume_other(s - 1)
        return carry

    lax.fori_loop(ahead + 1, nz, tail, 0)
    consume_other(nz - 1)

    def sent(zs, carry):
        src = zs * nx + x
        def left_z(k, i):
            @pl.when((zs <= z) & (z < nz - 1))
            def _():
                send(k, i, b + nx, up_sem.at[k, i]).wait_send()

            @pl.when((zs >= z) & (z > 0))
            def _():
                send(k, i, b - nx, dn_sem.at[k, i]).wait_send()

        for i in range(last + 1):
            left_z(src, i)
        left_z(zs * nx + (nx - 1 - x), last)
        for i in range(last):
            send(src, i, xb, x_sem.at[zs, i]).wait_send()

        @pl.when(zs == z)
        def _():
            send(src, last, xb, x_sem.at[zs, last]).wait_send()

        for v in range(nx):
            k = zs * nx + v

            @pl.when(k // per != g)
            def _():
                pltpu.make_async_remote_copy(
                    src_ref=ssend.at[k], dst_ref=srecv.at[0, 0], send_sem=s_ss.at[k],
                    recv_sem=s_rs.at[0, 0], device_id=(b, mate), device_id_type=MESH).wait_send()

        return carry

    lax.fori_loop(0, nz, sent, 0)
    for w in range(2):
        for d in range(ny):
            d_copy(d, w).wait_send()
        for d in range(1, ny):
            y_copy(d, w).wait_send()

    for p in range(per):
        for r in range(ng - 1):
            pltpu.make_async_remote_copy(
                src_ref=ssend.at[0], dst_ref=srecv.at[r, p], send_sem=s_ss.at[0],
                recv_sem=s_rs.at[r, p], device_id=(b, mate), device_id_type=MESH).wait_recv()
        for i in range(2):
            total = own[p, i]
            for r in range(ng - 1):
                total = total + srecv[r, p, i].astype(F32)
            out[i, :, p * rows : (p + 1) * rows] = total


def solution(mesh):
    nb, ng = mesh.shape["band"], mesh.shape["ga"]
    nx = 2
    nz = nb // nx
    ny = ng // 2
    per = nb // ng

    def step(elements, screened, energies, freq_points, freq_weights, band_of_slot):
        _, rows, depth = elements.shape
        quarter = screened.shape[3] // ng
        slots = energies.shape[0]
        any_space = pl.BlockSpec(memory_space=pl.ANY)
        vmem = pl.BlockSpec(memory_space=pltpu.VMEM)
        dma = pltpu.SemaphoreType.DMA
        result = pl.pallas_call(
            functools.partial(kernel, nb, ng, nx),
            out_shape=pltpu.VMEM((2, rows, per * rows), F32),
            in_specs=[any_space] * 6,
            out_specs=vmem,
            scratch_shapes=[
                pltpu.VMEM((slots,), F32), pltpu.VMEM((slots,), jnp.int32),
                pltpu.SMEM(freq_points.shape, F32), pltpu.SMEM(freq_weights.shape, F32), dma((4,)),
                pltpu.VMEM((2, nb * rows, depth), BF16),
                pltpu.VMEM((2, ng, 2, depth, quarter), BF16),
                pltpu.VMEM((2 * rows, 2 * depth), BF16),
                pltpu.VMEM((16, slots), BF16),
                pltpu.VMEM((nb, 2, rows), F32),
                pltpu.VMEM((ny, 2, 2 * rows, quarter), F32),
                pltpu.VMEM((ny, 2, 2 * rows, quarter), BF16),
                pltpu.VMEM((ny, 2, 2 * rows, quarter), BF16),
                pltpu.VMEM((ny - 1, 2, 2 * rows, quarter), BF16),
                pltpu.VMEM((ny - 1, 2, 2 * rows, quarter), BF16),
                pltpu.VMEM((2, 4 * rows, quarter), BF16),
                pltpu.VMEM((nb, 2, rows, rows), BF16),
                pltpu.VMEM((ng - 1, per, 2, rows, rows), BF16),
                pltpu.VMEM((per, 2, rows, rows), F32),
                dma, dma((2, ng)), dma((nb, 4)), dma((nb, 4)), dma((nz, 4)), dma((nb, 4)),
                dma((ny, 2)), dma((ny, 2)), dma((ny - 1, 2)), dma((ny - 1, 2)),
                dma((nb,)), dma((ng - 1, per)),
            ],
            compiler_params=pltpu.CompilerParams(
                collective_id=0, has_side_effects=True, vmem_limit_bytes=60 * 1024 * 1024),
        )(elements, screened, energies, band_of_slot, freq_points, freq_weights)
        return result

    placed = (P(None, "band", "ga"), P(None, None, "ga", None), P(), P(), P(), P())
    return jax.shard_map(
        step, mesh=mesh, in_specs=placed, out_specs=P(None, "band", "ga"), check_vma=False
    )
```

profile of v0, /device:TPU:0, one launch (start us, length us, event | category | flops | bytes accessed | tf_op | source)
XLA Modules:
  0.0 27.0 jit_solution(11146081069808483248)
XLA Ops:
  0.0 26.3 %shard_map.64 = f32[2,96,192]{2,1,0:T(8,128)S(1)} custom-call(bf16[2,96,512]{2,1,0:T(8,128)(2,1)} %el.1, bf16[2,2,512,2048]{3,2,1,0:T(8,128)(2,1)} %wh.1, f32[768]{0:T(1024)} %en_h.1, s32[768]{0:T(1024)} %bos_h.1, f32[2]{0:T(128)} %fp_h.1, f32[2]{0:T(128)} %fw_h.1), custom_call_target="tpu_custom_call" | custom-call | tf_op jit(solution)/shard_map/pallas_call | solution.py:357
  26.3 0.7 %copy.8 = f32[2,96,192]{2,1,0:T(8,128)} copy(f32[2,96,192]{2,1,0:T(8,128)S(1)} %shard_map.64) | data formatting | bytes 294912
where the time goes:
time: 27.1 us; the launch traced here: 27 us
  Pallas kernels  26.3 us (97%)
  local copies, waits for them, and re-layouts  0.68 us (3%)
    pallas_call x1, Pallas kernels, step(): pl.pallas_call(functools.partial(kernel, nb, ng, nx), out_shape=pltpu.VME...  26.3 us
    unnamed x1, local copies, waits for them, and re-layouts  0.68 us

commit v1 on v0

v1 whole, which is shorter than its diff:
```python
import functools

import jax
import jax.numpy as jnp
from jax import lax
from jax.experimental import pallas as pl
from jax.experimental.pallas import tpu as pltpu
from jax.sharding import PartitionSpec as P

MESH = pl.DeviceIdType.MESH
F32 = jnp.float32
BF16 = jnp.bfloat16
NT = (((1,), (1,)), ((), ()))
NX = 2
CHIPS = 4


def kernel(nb, ng, el, wh, en_h, bos_h, fp_h, fw_h, out, *scratch):
    (en, bos, fp, fw, mine, gat, wv, a_ref, e3, scr, held, dsend, drecv, ysend, yrecv, xsend, lv, lw, ssend, srecv, own,
     in_sem, loc_sem, w_sem, sw_ss, up_sem, dn_sem, g_recv, d_ss, d_rs, y_ss, y_rs, x_ss, x_rs, l_ss, l_rs, s_ss,
     s_rs) = scratch
    rows, depth = el.shape[1], el.shape[2]
    nz = nb // NX
    per = nb // ng
    slots = en.shape[0]
    b, g = lax.axis_index("band"), lax.axis_index("ga")
    z, x = b // NX, lax.rem(b, NX)
    y, c = g // 2, lax.rem(g, 2)
    mate = g + 1 - 2 * c
    across = lax.rem(g + 2, ng)
    xb = b + 1 - 2 * x
    straight = x == c
    crossed = x != c

    barrier = pltpu.get_barrier_semaphore()

    def greet(band, ga):
        pl.semaphore_signal(barrier, inc=1, device_id=(band, ga), device_id_type=MESH)

    @pl.when(z > 0)
    def _():
        greet(b - NX, g)

    @pl.when(z < nz - 1)
    def _():
        greet(b + NX, g)

    greet(xb, g)
    for r in range(1, ng):
        greet(b, lax.rem(g + r, ng))
        greet(xb, lax.rem(g + r, ng))

    small = [pltpu.make_async_copy(s, t, in_sem.at[i]) for i, (s, t) in enumerate(
        ((en_h, en), (bos_h, bos), (fp_h, fp), (fw_h, fw)))]
    local = pltpu.make_async_copy(el, mine, loc_sem.at[0])
    local.start()

    def placed():
        return pltpu.make_async_copy(el, gat.at[:, pl.ds(pl.multiple_of(z * rows, rows), rows), :], loc_sem.at[1])

    @pl.when(straight)
    def _():
        placed().start()

    for copy in small:
        copy.start()

    def slice_of(j):
        ys = 1 - y if j < 2 else y
        xs = x if j % 2 else 1 - x
        return ys * 2 + xs

    def w_copy(j, o):
        w = c if o else 1 - c
        cols = pl.ds(pl.multiple_of(slice_of(j) * depth, depth), depth)
        return pltpu.make_async_copy(wh.at[w, :, :, cols], wv.at[o, j], w_sem.at[o, j])

    order = ((0, 0), (1, 0), (0, 1), (1, 1), (2, 0), (3, 0), (2, 1), (3, 1))
    local.wait()

    @pl.when(straight)
    def _():
        placed().wait()

    below = jnp.where(z > 0, 1, 0)
    above = jnp.where(z < nz - 1, 1, 0)
    pl.semaphore_wait(barrier, 2 * ng - 1 + below + above)

    unit = rows // 6
    pieces = ((0, 2 * unit), (2 * unit, 2 * unit), (4 * unit, unit), (5 * unit, unit))
    parts = range(len(pieces))

    def block(zs, i):
        start, size = pieces[i]
        return gat.at[:, pl.ds(pl.multiple_of(zs * rows + start, unit), size), :]

    def send(zs, i, band, sem):
        ref = block(zs, i)
        return pltpu.make_async_remote_copy(
            src_ref=ref, dst_ref=ref, send_sem=sem, recv_sem=g_recv.at[zs, i], device_id=(band, g), device_id_type=MESH)

    def swap(i):
        start, size = pieces[i]
        return pltpu.make_async_remote_copy(
            src_ref=mine.at[:, pl.ds(start, size), :], dst_ref=block(z, i), send_sem=sw_ss.at[i],
            recv_sem=g_recv.at[z, i], device_id=(xb, mate), device_id_type=MESH)

    def arrived(zs, i):
        send(zs, i, b, up_sem.at[zs, i]).wait_recv()

    def send_z(zs, i, up, down):
        if up:
            @pl.when(z < nz - 1)
            def _():
                send(zs, i, b + NX, up_sem.at[zs, i]).start()

        if down:
            @pl.when(z > 0)
            def _():
                send(zs, i, b - NX, dn_sem.at[zs, i]).start()

    def fwd(s, which=parts):
        for i in which:
            for zs, up in ((z - s, True), (z + s, False)):
                @pl.when((zs >= 0) & (zs < nz))
                def _():
                    arrived(zs, i)
                    send_z(zs, i, up, not up)

    def swapped(which):
        @pl.when(crossed)
        def _():
            for i in which:
                arrived(z, i)
                send_z(z, i, True, True)

    @pl.when(straight)
    def _():
        for i in parts:
            send_z(z, i, True, True)

    @pl.when(crossed)
    def _():
        for i in parts:
            swap(i).start()

    for j, o in order:
        w_copy(j, o).start()

    for copy in small:
        copy.wait()
    row = lax.broadcasted_iota(jnp.int32, (16, slots), 0)
    e = en[...].reshape(1, slots)
    hi = e.astype(BF16).astype(F32)
    mid = (e - hi).astype(BF16).astype(F32)
    lo = e - hi - mid
    e3[...] = jnp.where(row == 0, hi, jnp.where(row == 1, mid, jnp.where(row == 2, lo, 0.0))).astype(BF16)
    tile = slots if slots <= 1024 else 8 * rows

    for u in range(slots // tile):
        slot = bos[u * tile : (u + 1) * tile].reshape(1, tile)

        def add(j, acc):
            at = pl.multiple_of(j * tile, tile)
            hit = lax.broadcasted_iota(jnp.int32, (tile, tile), 0) + at == slot
            return acc + jnp.dot(e3[:, pl.ds(at, tile)], jnp.where(hit, 1.0, 0.0).astype(BF16),
                                 preferred_element_type=F32)

        acc = lax.fori_loop(0, slots // tile, add, jnp.zeros((16, tile), F32))
        energy = jnp.sum(acc, axis=0, keepdims=True)
        for w in range(2):
            off = energy - fp[w]
            value = 0.5 * (fw[w] / (1.0 + 4.0 * off * off))
            for v in range(tile // rows):
                scr[u * (tile // rows) + v, w : w + 1, :] = value[:, v * rows : (v + 1) * rows]
    pick = lax.broadcasted_iota(jnp.int32, (rows, rows), 1) == lax.broadcasted_iota(
        jnp.int32, (rows, rows), 0)
    cols = [[jnp.sum(jnp.where(pick, scr[z * NX + v, w : w + 1, :], 0.0), axis=1, keepdims=True)
             for w in range(2)] for v in range(NX)]

    er = mine[0]
    ei = mine[1]
    a_ref[:rows, :depth] = er
    a_ref[:rows, depth:] = ei
    a_ref[rows:, :depth] = -ei
    a_ref[rows:, depth:] = er

    def d_copy(j):
        return pltpu.make_async_remote_copy(
            src_ref=dsend.at[j], dst_ref=drecv.at[j], send_sem=d_ss.at[j], recv_sem=d_rs.at[j],
            device_id=(b, mate), device_id_type=MESH)

    def y_copy(j, h):
        return pltpu.make_async_remote_copy(
            src_ref=ysend.at[j, h], dst_ref=yrecv.at[j, h], send_sem=y_ss.at[j, h], recv_sem=y_rs.at[j, h],
            device_id=(b, across), device_id_type=MESH)

    def x_copy(h):
        return pltpu.make_async_remote_copy(
            src_ref=xsend.at[h], dst_ref=lv.at[x, c, h], send_sem=x_ss.at[h], recv_sem=x_rs.at[h],
            device_id=(xb, g), device_id_type=MESH)

    def l_copy(v, band, h):
        ref = lv.at[band, c, h]
        return pltpu.make_async_remote_copy(
            src_ref=ref, dst_ref=ref, send_sem=l_ss.at[v, h], recv_sem=l_rs.at[v, h],
            device_id=(b, mate), device_id_type=MESH)

    def first(j, o):
        w_copy(j, o).wait()
        part = jnp.dot(a_ref[...], wv[o, j].reshape(2 * depth, depth), preferred_element_type=F32)
        if not o:
            dsend[j] = part.astype(BF16)
            d_copy(j).start()
            return
        d_copy(j).wait_recv()
        part = part + drecv[j].astype(F32)
        for h in range(2):
            if j < 2:
                ysend[j, h] = part[h * rows : (h + 1) * rows].astype(BF16)
                y_copy(j, h).start()
            else:
                held[j - 2, h] = part[h * rows : (h + 1) * rows]

    def to_x(h):
        y_copy(0, h).wait_recv()
        xsend[h] = (held[0, h] + yrecv[0, h].astype(F32)).astype(BF16)
        x_copy(h).start()

    def here(h):
        y_copy(1, h).wait_recv()
        lv[x, c, h] = (held[1, h] + yrecv[1, h].astype(F32)).astype(BF16)
        l_copy(0, x, h).start()

    def from_x(h):
        x_copy(h).wait_recv()
        l_copy(1, 1 - x, h).start()

    def consume_block(zs):
        at = pl.ds(pl.multiple_of(zs * rows, rows), rows)
        k = zs * NX + c
        pr = lax.dot_general(lv[...].reshape(8 * rows, depth), gat[0, at, :], NT, preferred_element_type=F32)
        pr = pr + lax.dot_general(lw[...].reshape(8 * rows, depth), gat[1, at, :], NT, preferred_element_type=F32)
        q, p = k // per, lax.rem(k, per)
        srow = [scr[k, w : w + 1, :] for w in range(2)]
        for v in range(NX):
            f = [cols[v][w] + srow[w] for w in range(2)]
            base = 4 * v * rows
            total = [f[0] * pr[base + i * rows : base + (i + 1) * rows]
                     + f[1] * pr[base + (2 + i) * rows : base + (3 + i) * rows] for i in range(2)]
            home = (q == g) & (x == v)

            @pl.when(home)
            def _():
                for i in range(2):
                    own[p, i] = total[i]
                    srecv[x * 2 + y, p, i] = jnp.zeros((rows, rows), BF16)

            @pl.when(jnp.logical_not(home))
            def _():
                for i in range(2):
                    ssend[zs, v, i] = total[i].astype(BF16)
                pltpu.make_async_remote_copy(
                    src_ref=ssend.at[zs, v], dst_ref=srecv.at[x * 2 + y, p], send_sem=s_ss.at[zs, v],
                    recv_sem=s_rs.at[x * 2 + y, p], device_id=(z * NX + v, q), device_id_type=MESH).start()

    def consume(s):
        @pl.when(z - s >= 0)
        def _():
            consume_block(z - s)

        if not (isinstance(s, int) and s == 0):
            @pl.when(z + s < nz)
            def _():
                consume_block(z + s)

    first(0, 0)
    first(1, 0)
    first(0, 1)
    first(1, 1)
    swapped((0, 1))
    first(2, 0)
    first(3, 0)
    swapped((2, 3))
    fwd(1, (0,))
    first(2, 1)
    first(3, 1)
    own[...] = jnp.zeros(own.shape, F32)
    fwd(1, (1,))
    to_x(0)
    fwd(1, (2, 3))
    to_x(1)
    fwd(2, (0,))
    from_x(0)
    fwd(2, (1,))
    here(0)
    from_x(1)
    fwd(2, (2, 3))
    here(1)
    fwd(3, (0,))
    for v in range(2):
        for h in range(2):
            l_copy(v, x, h).wait_recv()
    for v in range(NX):
        for w in range(2):
            lw[v, w, 0] = -lv[v, w, 1]
            lw[v, w, 1] = lv[v, w, 0]
    consume(0)
    consume(1)
    fwd(3, (1,))
    consume(2)
    fwd(3, (2, 3))
    consume(3)

    def tail(s, carry):
        fwd(s)
        consume(s)
        return carry

    lax.fori_loop(4, nz, tail, 0)

    chip = x * 2 + y
    for p in range(per):
        for r in range(CHIPS):
            @pl.when(jnp.logical_not((chip == r) & (c == p % 2)))
            def _():
                pltpu.make_async_remote_copy(
                    src_ref=ssend.at[0, 0], dst_ref=srecv.at[r, p], send_sem=s_ss.at[0, 0], recv_sem=s_rs.at[r, p],
                    device_id=(b, mate), device_id_type=MESH).wait_recv()
        for i in range(2):
            total = own[p, i]
            for r in range(CHIPS):
                total = total + srecv[r, p, i].astype(F32)
            out[i, :, p * rows : (p + 1) * rows] = total

    def sent(zs, carry):
        for i in parts:
            @pl.when((zs <= z) & (z < nz - 1))
            def _():
                send(zs, i, b, up_sem.at[zs, i]).wait_send()

            @pl.when((zs >= z) & (z > 0))
            def _():
                send(zs, i, b, dn_sem.at[zs, i]).wait_send()

        q = (zs * NX + c) // per
        for v in range(NX):
            @pl.when((q != g) | (x != v))
            def _():
                pltpu.make_async_remote_copy(
                    src_ref=ssend.at[zs, v], dst_ref=srecv.at[0, 0], send_sem=s_ss.at[zs, v], recv_sem=s_rs.at[0, 0],
                    device_id=(b, mate), device_id_type=MESH).wait_send()

        return carry

    lax.fori_loop(0, nz, sent, 0)

    @pl.when(crossed)
    def _():
        for i in parts:
            swap(i).wait_send()

    for j in range(4):
        d_copy(j).wait_send()
    for h in range(2):
        for j in range(2):
            y_copy(j, h).wait_send()
            l_copy(j, x, h).wait_send()
        x_copy(h).wait_send()


def solution(mesh):
    nb, ng = mesh.shape["band"], mesh.shape["ga"]
    nz = nb // NX
    per = nb // ng

    def step(elements, screened, energies, freq_points, freq_weights, band_of_slot):
        _, rows, depth = elements.shape
        slots = energies.shape[0]
        any_space = pl.BlockSpec(memory_space=pl.ANY)
        vmem = pl.BlockSpec(memory_space=pltpu.VMEM)
        dma = pltpu.SemaphoreType.DMA
        return pl.pallas_call(
            functools.partial(kernel, nb, ng),
            out_shape=pltpu.VMEM((2, rows, per * rows), F32),
            in_specs=[any_space] * 6,
            out_specs=vmem,
            scratch_shapes=[
                pltpu.VMEM((slots,), F32), pltpu.VMEM((slots,), jnp.int32),
                pltpu.SMEM(freq_points.shape, F32), pltpu.SMEM(freq_weights.shape, F32),
                pltpu.VMEM((2, rows, depth), BF16),
                pltpu.VMEM((2, nz * rows, depth), BF16),
                pltpu.VMEM((2, 4, 2, depth, depth), BF16),
                pltpu.VMEM((2 * rows, 2 * depth), BF16),
                pltpu.VMEM((16, slots), BF16),
                pltpu.VMEM((nb, 2, rows), F32),
                pltpu.VMEM((2, 2, rows, depth), F32),
                pltpu.VMEM((4, 2 * rows, depth), BF16),
                pltpu.VMEM((4, 2 * rows, depth), BF16),
                pltpu.VMEM((2, 2, rows, depth), BF16),
                pltpu.VMEM((2, 2, rows, depth), BF16),
                pltpu.VMEM((2, rows, depth), BF16),
                pltpu.VMEM((NX, 2, 2, rows, depth), BF16),
                pltpu.VMEM((NX, 2, 2, rows, depth), BF16),
                pltpu.VMEM((nz, NX, 2, rows, rows), BF16),
                pltpu.VMEM((CHIPS, per, 2, rows, rows), BF16),
                pltpu.VMEM((per, 2, rows, rows), F32),
                dma((4,)), dma((2,)), dma((2, 4)), dma((4,)), dma((nz, 4)), dma((nz, 4)), dma((nz, 4)),
                dma((4,)), dma((4,)), dma((2, 2)), dma((2, 2)), dma((2,)), dma((2,)), dma((2, 2)), dma((2, 2)),
                dma((nz, NX)), dma((CHIPS, per)),
            ],
            compiler_params=pltpu.CompilerParams(
                collective_id=0, has_side_effects=True, vmem_limit_bytes=60 * 1024 * 1024),
        )(elements, screened, energies, band_of_slot, freq_points, freq_weights)

    placed = (P(None, "band", "ga"), P(None, None, "ga", None), P(), P(), P(), P())
    return jax.shard_map(
        step, mesh=mesh, in_specs=placed, out_specs=P(None, "band", "ga"), check_vma=False
    )
```

time: 27.1 us -> 27.8 us (1.026)
  the two profiles are of different devices: /device:TPU:0 before, /device:TPU:5 now
where the time goes in v1:
time: 27.8 us; the launch traced here: 27.4 us
  Pallas kernels  26.7 us (96%)
  local copies, waits for them, and re-layouts  0.68 us (2%)
    pallas_call x1, Pallas kernels, step(): pl.pallas_call(functools.partial(kernel, nb, ng), out_shape=pltpu.VMEM((2...  26.7 us
    unnamed x1, local copies, waits for them, and re-layouts  0.68 us

profile of v1, /device:TPU:5, one launch (start us, length us, event | category | flops | bytes accessed | tf_op | source)
XLA Modules:
  0.0 27.4 jit_solution(8808329073440118193)
XLA Ops:
  0.0 26.7 %shard_map.64 = f32[2,96,192]{2,1,0:T(8,128)S(1)} custom-call(bf16[2,96,512]{2,1,0:T(8,128)(2,1)} %el.1, bf16[2,2,512,2048]{3,2,1,0:T(8,128)(2,1)} %wh.1, f32[768]{0:T(1024)} %en_h.1, s32[768]{0:T(1024)} %bos_h.1, f32[2]{0:T(128)} %fp_h.1, f32[2]{0:T(128)} %fw_h.1), custom_call_target="tpu_custom_call" | custom-call | tf_op jit(solution)/shard_map/pallas_call | solution.py:383
  26.7 0.7 %copy.8 = f32[2,96,192]{2,1,0:T(8,128)} copy(f32[2,96,192]{2,1,0:T(8,128)S(1)} %shard_map.64) | data formatting | bytes 294912

commit v2 on v1

v2 whole, which is shorter than its diff:
```python
import functools

import jax
import jax.numpy as jnp
from jax import lax
from jax.experimental import pallas as pl
from jax.experimental.pallas import tpu as pltpu
from jax.sharding import PartitionSpec as P

MESH = pl.DeviceIdType.MESH
F32 = jnp.float32
BF16 = jnp.bfloat16
NT = (((1,), (1,)), ((), ()))
NX = 2
CUTS = 4
LANES = 128
CHIPS = 4


def packs(rows):
    return 2 * (2 * rows - LANES) == LANES


def pack(re, im):
    rows = re.shape[0]
    if not packs(rows):
        return jnp.concatenate([re, im], axis=0)
    spare = LANES - rows
    top = jnp.concatenate([re, im[:, :spare]], axis=1)
    rest = im[:, spare:]
    return jnp.concatenate([top, jnp.concatenate([rest[: rows // 2], rest[rows // 2 :]], axis=1)], axis=0)


def unpack(both, rows):
    if not packs(rows):
        return both[:rows], both[rows:]
    rest = both[rows:]
    rest = jnp.concatenate([rest[:, : LANES // 2], rest[:, LANES // 2 :]], axis=0)
    return both[:rows, :rows], jnp.concatenate([both[:rows, rows:], rest], axis=1)


def kernel(nb, ng, el, wh, en_h, bos_h, fp_h, fw_h, out, *scratch):
    (en, bos, fp, fw, mine, gat, wv, a_ref, e3, scr, held, dsend, drecv, ysend, yrecv, xsend, lv, lw, ssend, srecv, own,
     in_sem, loc_sem, w_sem, sw_ss, up_sem, dn_sem, g_recv, d_ss, d_rs, y_ss, y_rs, x_ss, x_rs, l_ss, l_rs, s_ss,
     s_rs) = scratch
    rows, depth = el.shape[1], el.shape[2]
    nz = nb // NX
    pad = gat.shape[1] // nz
    cut = 2 * rows // CUTS
    per = nb // ng
    slots = en.shape[0]
    b, g = lax.axis_index("band"), lax.axis_index("ga")
    z, x = b // NX, lax.rem(b, NX)
    y, c = g // 2, lax.rem(g, 2)
    mate = g + 1 - 2 * c
    across = lax.rem(g + 2, ng)
    xb = b + 1 - 2 * x
    straight = x == c
    crossed = x != c

    barrier = pltpu.get_barrier_semaphore()

    def greet(band, ga):
        pl.semaphore_signal(barrier, inc=1, device_id=(band, ga), device_id_type=MESH)

    @pl.when(z > 0)
    def _():
        greet(b - NX, g)

    @pl.when(z < nz - 1)
    def _():
        greet(b + NX, g)

    greet(xb, g)
    greet(xb, mate)
    for r in range(1, ng):
        greet(b, lax.rem(g + r, ng))

    small = [pltpu.make_async_copy(s, t, in_sem.at[i]) for i, (s, t) in enumerate(
        ((en_h, en), (bos_h, bos), (fp_h, fp), (fw_h, fw)))]
    local = pltpu.make_async_copy(el, mine, loc_sem.at[0])
    local.start()

    def placed():
        return pltpu.make_async_copy(el, gat.at[:, pl.ds(pl.multiple_of(z * pad, pad), rows), :], loc_sem.at[1])

    @pl.when(straight)
    def _():
        placed().start()

    for copy in small:
        copy.start()

    def slice_of(j):
        ys = 1 - y if j < 2 else y
        xs = x if j % 2 else 1 - x
        return ys * 2 + xs

    def w_copy(j, o):
        w = c if o else 1 - c
        cols = pl.ds(pl.multiple_of(slice_of(j) * depth, depth), depth)
        return pltpu.make_async_copy(wh.at[w, :, :, cols], wv.at[o, j], w_sem.at[o, j])

    order = ((0, 0), (1, 0), (0, 1), (1, 1), (2, 0), (3, 0), (2, 1), (3, 1))
    for j, o in order:
        w_copy(j, o).start()
    local.wait()

    @pl.when(straight)
    def _():
        placed().wait()

    below = jnp.where(z > 0, 1, 0)
    above = jnp.where(z < nz - 1, 1, 0)
    pl.semaphore_wait(barrier, ng + 1 + below + above)

    unit = rows // 6
    pieces = ((0, 2 * unit), (2 * unit, 2 * unit), (4 * unit, unit), (5 * unit, unit))
    parts = range(len(pieces))

    def block(zs, i):
        start, size = pieces[i]
        return gat.at[:, pl.ds(pl.multiple_of(zs * pad + start, unit), size), :]

    def send(zs, i, band, sem):
        ref = block(zs, i)
        return pltpu.make_async_remote_copy(
            src_ref=ref, dst_ref=ref, send_sem=sem, recv_sem=g_recv.at[zs, i], device_id=(band, g), device_id_type=MESH)

    def swap(i):
        start, size = pieces[i]
        return pltpu.make_async_remote_copy(
            src_ref=mine.at[:, pl.ds(start, size), :], dst_ref=block(z, i), send_sem=sw_ss.at[i],
            recv_sem=g_recv.at[z, i], device_id=(xb, mate), device_id_type=MESH)

    def arrived(zs, i):
        send(zs, i, b, up_sem.at[zs, i]).wait_recv()

    def send_z(zs, i, up, down):
        if up:
            @pl.when(z < nz - 1)
            def _():
                send(zs, i, b + NX, up_sem.at[zs, i]).start()

        if down:
            @pl.when(z > 0)
            def _():
                send(zs, i, b - NX, dn_sem.at[zs, i]).start()

    def fwd(s, which=parts):
        for i in which:
            for zs, up in ((z - s, True), (z + s, False)):
                @pl.when((zs >= 0) & (zs < nz))
                def _():
                    arrived(zs, i)
                    send_z(zs, i, up, not up)

    def swapped(which):
        @pl.when(crossed)
        def _():
            for i in which:
                arrived(z, i)
                send_z(z, i, True, True)

    @pl.when(straight)
    def _():
        for i in parts:
            send_z(z, i, True, True)

    @pl.when(crossed)
    def _():
        for i in parts:
            swap(i).start()

    er = mine[0]
    ei = mine[1]
    a_ref[:rows, :depth] = er
    a_ref[:rows, depth:] = ei
    a_ref[rows:, :depth] = -ei
    a_ref[rows:, depth:] = er

    def d_copy(j):
        return pltpu.make_async_remote_copy(
            src_ref=dsend.at[j], dst_ref=drecv.at[j], send_sem=d_ss.at[j], recv_sem=d_rs.at[j],
            device_id=(b, mate), device_id_type=MESH)

    def y_copy(j, h):
        return pltpu.make_async_remote_copy(
            src_ref=ysend.at[j, h], dst_ref=yrecv.at[j, h], send_sem=y_ss.at[j, h], recv_sem=y_rs.at[j, h],
            device_id=(b, across), device_id_type=MESH)

    def x_copy(h):
        return pltpu.make_async_remote_copy(
            src_ref=xsend.at[h], dst_ref=lv.at[x, c, h], send_sem=x_ss.at[h], recv_sem=x_rs.at[h],
            device_id=(xb, g), device_id_type=MESH)

    def l_copy(v, band, h):
        ref = lv.at[band, c, h]
        return pltpu.make_async_remote_copy(
            src_ref=ref, dst_ref=ref, send_sem=l_ss.at[v, h], recv_sem=l_rs.at[v, h],
            device_id=(b, mate), device_id_type=MESH)

    def first(j, o):
        w_copy(j, o).wait()
        part = jnp.dot(a_ref[...], wv[o, j].reshape(2 * depth, depth), preferred_element_type=F32)
        if not o:
            dsend[j] = part.astype(BF16)
            d_copy(j).start()
            return
        d_copy(j).wait_recv()
        part = part + drecv[j].astype(F32)
        for h in range(CUTS):
            if j < 2:
                ysend[j, h] = part[h * cut : (h + 1) * cut].astype(BF16)
                y_copy(j, h).start()
            else:
                held[j - 2, h] = part[h * cut : (h + 1) * cut]

    def to_x(h):
        y_copy(0, h).wait_recv()
        xsend[h] = (held[0, h] + yrecv[0, h].astype(F32)).astype(BF16)
        x_copy(h).start()

    def here(h):
        y_copy(1, h).wait_recv()
        lv[x, c, h] = (held[1, h] + yrecv[1, h].astype(F32)).astype(BF16)
        l_copy(0, x, h).start()

    def from_x(h):
        x_copy(h).wait_recv()
        l_copy(1, 1 - x, h).start()

    def ready():
        for other in range(NX):
            for h in range(CUTS):
                l_copy(other, x, h).wait_recv()
        half = CUTS // 2
        for v in range(NX):
            for w in range(2):
                lw[v, w, :half] = -lv[v, w, half:]
                lw[v, w, half:] = lv[v, w, :half]

    def consume(zs, count):
        at = pl.ds(pl.multiple_of(zs * pad, pad), count * pad)
        pr = lax.dot_general(lv[...].reshape(8 * rows, depth), gat[0, at, :], NT, preferred_element_type=F32)
        pr = pr + lax.dot_general(lw[...].reshape(8 * rows, depth), gat[1, at, :], NT, preferred_element_type=F32)
        for t in range(count):
            scale_and_send(zs + t, pr[:, t * pad : t * pad + rows])

    def scale_and_send(zs, pr):
        k = zs * NX + c
        q, p = k // per, lax.rem(k, per)
        srow = [scr[k, w : w + 1, :] for w in range(2)]
        for v in range(NX):
            f = [cols[v][w] + srow[w] for w in range(2)]
            each = [pr[(4 * v + i) * rows : (4 * v + i + 1) * rows] for i in range(4)]
            total = pack(*[f[0] * each[i] + f[1] * each[2 + i] for i in range(2)])
            home = (q == g) & (x == v)

            @pl.when(home)
            def _():
                own[p] = total
                srecv[x * 2 + y, p] = jnp.zeros(total.shape, BF16)

            @pl.when(jnp.logical_not(home))
            def _():
                ssend[zs, v] = total.astype(BF16)
                pltpu.make_async_remote_copy(
                    src_ref=ssend.at[zs, v], dst_ref=srecv.at[x * 2 + y, p], send_sem=s_ss.at[zs, v],
                    recv_sem=s_rs.at[x * 2 + y, p], device_id=(z * NX + v, q), device_id_type=MESH).start()

    first(0, 0)
    first(1, 0)

    for copy in small:
        copy.wait()
    row = lax.broadcasted_iota(jnp.int32, (16, slots), 0)
    e = en[...].reshape(1, slots)
    hi = e.astype(BF16).astype(F32)
    mid = (e - hi).astype(BF16).astype(F32)
    lo = e - hi - mid
    e3[...] = jnp.where(row == 0, hi, jnp.where(row == 1, mid, jnp.where(row == 2, lo, 0.0))).astype(BF16)
    tile = slots if slots <= 1024 else 8 * rows

    for u in range(slots // tile):
        slot = bos[u * tile : (u + 1) * tile].reshape(1, tile)

        def add(j, acc):
            at = pl.multiple_of(j * tile, tile)
            hit = lax.broadcasted_iota(jnp.int32, (tile, tile), 0) + at == slot
            return acc + jnp.dot(e3[:, pl.ds(at, tile)], jnp.where(hit, 1.0, 0.0).astype(BF16),
                                 preferred_element_type=F32)

        acc = lax.fori_loop(0, slots // tile, add, jnp.zeros((16, tile), F32))
        energy = jnp.sum(acc, axis=0, keepdims=True)
        for w in range(2):
            off = energy - fp[w]
            value = 0.5 * (fw[w] / (1.0 + 4.0 * off * off))
            for v in range(tile // rows):
                scr[u * (tile // rows) + v, w : w + 1, :] = value[:, v * rows : (v + 1) * rows]
    pick = lax.broadcasted_iota(jnp.int32, (rows, rows), 1) == lax.broadcasted_iota(
        jnp.int32, (rows, rows), 0)
    cols = [[jnp.sum(jnp.where(pick, scr[band, w : w + 1, :], 0.0), axis=1, keepdims=True)
             for w in range(2)] for band in (z * NX, z * NX + 1)]

    first(0, 1)
    first(1, 1)
    first(2, 0)
    first(3, 0)
    swapped((0, 1))
    first(2, 1)
    swapped((2, 3))
    first(3, 1)
    own[...] = jnp.zeros(own.shape, F32)

    @pl.when(straight)
    def _():
        fwd(1, (0, 1))
        to_x(0)
        fwd(1, (2, 3))
        to_x(1)
        to_x(2)
        fwd(2, (0,))
        to_x(3)
        fwd(2, (1,))
        here(0)
        from_x(0)
        fwd(2, (2,))
        here(1)
        from_x(1)
        fwd(2, (3,))

    @pl.when(crossed)
    def _():
        to_x(0)
        to_x(1)
        fwd(1, (0, 1))
        to_x(2)
        fwd(1, (2,))
        to_x(3)
        fwd(1, (3,))
        here(0)
        from_x(0)
        fwd(2, (0,))
        here(1)
        from_x(1)
        fwd(2, (1,))

    here(2)
    from_x(2)
    here(3)
    from_x(3)

    @pl.when(crossed)
    def _():
        fwd(2, (2, 3))

    ready()
    consume(z // 2 * 2, 2)

    def tail(t, carry):
        for near, far in ((2 * (z // 2 - t) + 1, 2 * (z // 2 - t)), (2 * (z // 2 + t), 2 * (z // 2 + t) + 1)):
            @pl.when((near >= 0) & (near < nz))
            def _():
                consume(near, 1)

        fwd(2 * t + 1)
        for near, far in ((2 * (z // 2 - t) + 1, 2 * (z // 2 - t)), (2 * (z // 2 + t), 2 * (z // 2 + t) + 1)):
            @pl.when((near >= 0) & (near < nz))
            def _():
                consume(far, 1)

        @pl.when(2 * t + 2 < nz)
        def _():
            fwd(2 * t + 2)

        return carry

    lax.fori_loop(1, nz // 2, tail, 0)

    chip = x * 2 + y
    for p in range(per):
        for r in range(CHIPS):
            @pl.when(jnp.logical_not((chip == r) & (c == p % 2)))
            def _():
                pltpu.make_async_remote_copy(
                    src_ref=ssend.at[0, 0], dst_ref=srecv.at[r, p], send_sem=s_ss.at[0, 0], recv_sem=s_rs.at[r, p],
                    device_id=(b, mate), device_id_type=MESH).wait_recv()
        total = own[p]
        for r in range(CHIPS):
            total = total + srecv[r, p].astype(F32)
        for i, each in enumerate(unpack(total, rows)):
            out[i, :, p * rows : (p + 1) * rows] = each

    def sent(zs, carry):
        for i in parts:
            @pl.when((zs <= z) & (z < nz - 1))
            def _():
                send(zs, i, b, up_sem.at[zs, i]).wait_send()

            @pl.when((zs >= z) & (z > 0))
            def _():
                send(zs, i, b, dn_sem.at[zs, i]).wait_send()

        q = (zs * NX + c) // per
        for v in range(NX):
            @pl.when((q != g) | (x != v))
            def _():
                pltpu.make_async_remote_copy(
                    src_ref=ssend.at[zs, v], dst_ref=srecv.at[0, 0], send_sem=s_ss.at[zs, v], recv_sem=s_rs.at[0, 0],
                    device_id=(b, mate), device_id_type=MESH).wait_send()

        return carry

    lax.fori_loop(0, nz, sent, 0)

    @pl.when(crossed)
    def _():
        for i in parts:
            swap(i).wait_send()

    for j in range(4):
        d_copy(j).wait_send()
    for h in range(CUTS):
        for j in range(2):
            y_copy(j, h).wait_send()
            l_copy(j, x, h).wait_send()
        x_copy(h).wait_send()


def solution(mesh):
    nb, ng = mesh.shape["band"], mesh.shape["ga"]
    nz = nb // NX
    per = nb // ng

    def step(elements, screened, energies, freq_points, freq_weights, band_of_slot):
        _, rows, depth = elements.shape
        slots = energies.shape[0]
        pad = -(-rows // 128) * 128
        cut = 2 * rows // CUTS
        packed = (3 * rows // 2, LANES) if packs(rows) else (2 * rows, rows)
        any_space = pl.BlockSpec(memory_space=pl.ANY)
        vmem = pl.BlockSpec(memory_space=pltpu.VMEM)
        dma = pltpu.SemaphoreType.DMA
        return pl.pallas_call(
            functools.partial(kernel, nb, ng),
            out_shape=pltpu.VMEM((2, rows, per * rows), F32),
            in_specs=[any_space] * 6,
            out_specs=vmem,
            scratch_shapes=[
                pltpu.VMEM((slots,), F32), pltpu.VMEM((slots,), jnp.int32),
                pltpu.SMEM(freq_points.shape, F32), pltpu.SMEM(freq_weights.shape, F32),
                pltpu.VMEM((2, rows, depth), BF16),
                pltpu.VMEM((2, nz * pad, depth), BF16),
                pltpu.VMEM((2, 4, 2, depth, depth), BF16),
                pltpu.VMEM((2 * rows, 2 * depth), BF16),
                pltpu.VMEM((16, slots), BF16),
                pltpu.VMEM((nb, 2, rows), F32),
                pltpu.VMEM((2, CUTS, cut, depth), F32),
                pltpu.VMEM((4, 2 * rows, depth), BF16),
                pltpu.VMEM((4, 2 * rows, depth), BF16),
                pltpu.VMEM((2, CUTS, cut, depth), BF16),
                pltpu.VMEM((2, CUTS, cut, depth), BF16),
                pltpu.VMEM((CUTS, cut, depth), BF16),
                pltpu.VMEM((NX, 2, CUTS, cut, depth), BF16),
                pltpu.VMEM((NX, 2, CUTS, cut, depth), BF16),
                pltpu.VMEM((nz, NX) + packed, BF16),
                pltpu.VMEM((CHIPS, per) + packed, BF16),
                pltpu.VMEM((per,) + packed, F32),
                dma((4,)), dma((2,)), dma((2, 4)), dma((4,)), dma((nz, 4)), dma((nz, 4)), dma((nz, 4)),
                dma((4,)), dma((4,)), dma((2, CUTS)), dma((2, CUTS)), dma((CUTS,)), dma((CUTS,)), dma((2, CUTS)), dma((2, CUTS)),
                dma((nz, NX)), dma((CHIPS, per)),
            ],
            compiler_params=pltpu.CompilerParams(
                collective_id=0, has_side_effects=True, vmem_limit_bytes=60 * 1024 * 1024),
        )(elements, screened, energies, band_of_slot, freq_points, freq_weights)

    placed = (P(None, "band", "ga"), P(None, None, "ga", None), P(), P(), P(), P())
    return jax.shard_map(
        step, mesh=mesh, in_specs=placed, out_specs=P(None, "band", "ga"), check_vma=False
    )
```

time: 27.8 us -> 26.5 us (0.953)
  Pallas kernels: 26.7 us -> 25.6 us
    pallas_call x1, Pallas kernels: 26.7 us -> 25.6 us  [step(): pl.pallas_call(functools.partial(kernel, nb, ng), out_shape=pltpu.VMEM((2...]
where the time goes in v2:
time: 26.5 us; the launch traced here: 26.3 us
  Pallas kernels  25.6 us (97%)
  local copies, waits for them, and re-layouts  0.68 us (3%)
    pallas_call x1, Pallas kernels, step(): pl.pallas_call(functools.partial(kernel, nb, ng), out_shape=pltpu.VMEM((2...  25.6 us
    unnamed x1, local copies, waits for them, and re-layouts  0.68 us

profile of v2, /device:TPU:5, one launch (start us, length us, event | category | flops | bytes accessed | tf_op | source)
XLA Modules:
  0.0 26.3 jit_solution(7841911804082729874)
XLA Ops:
  0.0 25.6 %shard_map.64 = f32[2,96,192]{2,1,0:T(8,128)S(1)} custom-call(bf16[2,96,512]{2,1,0:T(8,128)(2,1)} %el.1, bf16[2,2,512,2048]{3,2,1,0:T(8,128)(2,1)} %wh.1, f32[768]{0:T(1024)} %en_h.1, s32[768]{0:T(1024)} %bos_h.1, f32[2]{0:T(128)} %fp_h.1, f32[2]{0:T(128)} %fw_h.1), custom_call_target="tpu_custom_call" | custom-call | tf_op jit(solution)/shard_map/pallas_call | solution.py:445
  25.6 0.7 %copy.8 = f32[2,96,192]{2,1,0:T(8,128)} copy(f32[2,96,192]{2,1,0:T(8,128)S(1)} %shard_map.64) | data formatting | bytes 294912

commit v3 on v2

--- a/solution.py
+++ b/solution.py
@@ -92,8 +92,8 @@
         copy.start()
 
     def slice_of(j):
-        ys = 1 - y if j < 2 else y
-        xs = x if j % 2 else 1 - x
+        ys = lax.rem(y + 1 - j // 2, 2)
+        xs = lax.rem(x + 1 + j, 2)
         return ys * 2 + xs
 
     def w_copy(j, o):
@@ -101,9 +101,12 @@
         cols = pl.ds(pl.multiple_of(slice_of(j) * depth, depth), depth)
         return pltpu.make_async_copy(wh.at[w, :, :, cols], wv.at[o, j], w_sem.at[o, j])
 
-    order = ((0, 0), (1, 0), (0, 1), (1, 1), (2, 0), (3, 0), (2, 1), (3, 1))
-    for j, o in order:
-        w_copy(j, o).start()
+    def load(j, carry):
+        for o in range(2):
+            w_copy(j, o).start()
+        return carry
+
+    lax.fori_loop(0, 4, load, 0)
     local.wait()
 
     @pl.when(straight)

time: 26.5 us -> 24.9 us (0.940)
  Pallas kernels: 25.6 us -> 24.1 us
    pallas_call x1, Pallas kernels: 25.6 us -> 24.1 us  [step(): pl.pallas_call(functools.partial(kernel, nb, ng), out_shape=pltpu.VMEM((2...]
where the time goes in v3:
time: 24.9 us; the launch traced here: 24.8 us
  Pallas kernels  24.1 us (97%)
  local copies, waits for them, and re-layouts  0.68 us (3%)
    pallas_call x1, Pallas kernels, step(): pl.pallas_call(functools.partial(kernel, nb, ng), out_shape=pltpu.VMEM((2...  24.1 us
    unnamed x1, local copies, waits for them, and re-layouts  0.68 us

profile of v3, /device:TPU:5, one launch (start us, length us, event | category | flops | bytes accessed | tf_op | source)
XLA Modules:
  0.0 24.8 jit_solution(7972293625562798214)
XLA Ops:
  0.0 24.1 %shard_map.64 = f32[2,96,192]{2,1,0:T(8,128)S(1)} custom-call(bf16[2,96,512]{2,1,0:T(8,128)(2,1)} %el.1, bf16[2,2,512,2048]{3,2,1,0:T(8,128)(2,1)} %wh.1, f32[768]{0:T(1024)} %en_h.1, s32[768]{0:T(1024)} %bos_h.1, f32[2]{0:T(128)} %fp_h.1, f32[2]{0:T(128)} %fw_h.1), custom_call_target="tpu_custom_call" | custom-call | tf_op jit(solution)/shard_map/pallas_call | solution.py:448
  24.1 0.7 %copy.8 = f32[2,96,192]{2,1,0:T(8,128)} copy(f32[2,96,192]{2,1,0:T(8,128)S(1)} %shard_map.64) | data formatting | bytes 294912

commit v4 on v3

--- a/solution.py
+++ b/solution.py
@@ -150,9 +150,11 @@
             def _():
                 send(zs, i, b - NX, dn_sem.at[zs, i]).start()
 
-    def fwd(s, which=parts):
+    def fwd(s, which=parts, ways=(True, False)):
         for i in which:
-            for zs, up in ((z - s, True), (z + s, False)):
+            for up in ways:
+                zs = z - s if up else z + s
+
                 @pl.when((zs >= 0) & (zs < nz))
                 def _():
                     arrived(zs, i)
@@ -164,6 +166,11 @@
             for i in which:
                 arrived(z, i)
                 send_z(z, i, True, True)
+
+    def early(which):
+        @pl.when(straight)
+        def _():
+            fwd(1, which, (True,))
 
     @pl.when(straight)
     def _():
@@ -233,44 +240,46 @@
         x_copy(h).wait_recv()
         l_copy(1, 1 - x, h).start()
 
-    def ready():
-        for other in range(NX):
-            for h in range(CUTS):
-                l_copy(other, x, h).wait_recv()
+    def ready(other):
         half = CUTS // 2
-        for v in range(NX):
-            for w in range(2):
-                lw[v, w, :half] = -lv[v, w, half:]
-                lw[v, w, half:] = lv[v, w, :half]
-
-    def consume(zs, count):
+        v = 1 - x if other else x
+        for h in range(CUTS):
+            l_copy(other, x, h).wait_recv()
+        for w in range(2):
+            lw[v, w, :half] = -lv[v, w, half:]
+            lw[v, w, half:] = lv[v, w, :half]
+
+    def consume(zs, count, v=None):
         at = pl.ds(pl.multiple_of(zs * pad, pad), count * pad)
-        pr = lax.dot_general(lv[...].reshape(8 * rows, depth), gat[0, at, :], NT, preferred_element_type=F32)
-        pr = pr + lax.dot_general(lw[...].reshape(8 * rows, depth), gat[1, at, :], NT, preferred_element_type=F32)
+        bands = range(NX) if v is None else (v,)
+        left, right = [ref[...] if v is None else ref[v] for ref in (lv, lw)]
+        shape = (4 * len(bands) * rows, depth)
+        pr = lax.dot_general(left.reshape(shape), gat[0, at, :], NT, preferred_element_type=F32)
+        pr = pr + lax.dot_general(right.reshape(shape), gat[1, at, :], NT, preferred_element_type=F32)
         for t in range(count):
-            scale_and_send(zs + t, pr[:, t * pad : t * pad + rows])
-
-    def scale_and_send(zs, pr):
+            for n, band in enumerate(bands):
+                scale_and_send(zs + t, band, [
+                    pr[(4 * n + i) * rows : (4 * n + i + 1) * rows, t * pad : t * pad + rows] for i in range(4)])
+
+    def scale_and_send(zs, v, each):
         k = zs * NX + c
         q, p = k // per, lax.rem(k, per)
-        srow = [scr[k, w : w + 1, :] for w in range(2)]
-        for v in range(NX):
-            f = [cols[v][w] + srow[w] for w in range(2)]
-            each = [pr[(4 * v + i) * rows : (4 * v + i + 1) * rows] for i in range(4)]
-            total = pack(*[f[0] * each[i] + f[1] * each[2 + i] for i in range(2)])
-            home = (q == g) & (x == v)
-
-            @pl.when(home)
-            def _():
-                own[p] = total
-                srecv[x * 2 + y, p] = jnp.zeros(total.shape, BF16)
-
-            @pl.when(jnp.logical_not(home))
-            def _():
-                ssend[zs, v] = total.astype(BF16)
-                pltpu.make_async_remote_copy(
-                    src_ref=ssend.at[zs, v], dst_ref=srecv.at[x * 2 + y, p], send_sem=s_ss.at[zs, v],
-                    recv_sem=s_rs.at[x * 2 + y, p], device_id=(z * NX + v, q), device_id_type=MESH).start()
+        col = [jnp.where(v == 0, cols[0][w], cols[1][w]) for w in range(2)]
+        f = [col[w] + scr[k, w : w + 1, :] for w in range(2)]
+        total = [f[0] * each[i] + f[1] * each[2 + i] for i in range(2)]
+        home = (q == g) & (x == v)
+
+        @pl.when(home)
+        def _():
+            own[p] = pack(*total)
+            srecv[x * 2 + y, p] = jnp.zeros(srecv.shape[2:], BF16)
+
+        @pl.when(jnp.logical_not(home))
+        def _():
+            ssend[zs, v] = pack(*[part.astype(BF16) for part in total])
+            pltpu.make_async_remote_copy(
+                src_ref=ssend.at[zs, v], dst_ref=srecv.at[x * 2 + y, p], send_sem=s_ss.at[zs, v],
+                recv_sem=s_rs.at[x * 2 + y, p], device_id=(z * NX + v, q), device_id_type=MESH).start()
 
     first(0, 0)
     first(1, 0)
@@ -309,23 +318,23 @@
     first(0, 1)
     first(1, 1)
     first(2, 0)
+    swapped((0,))
     first(3, 0)
-    swapped((0, 1))
+    swapped((1, 2, 3))
+    early((0, 1))
     first(2, 1)
-    swapped((2, 3))
     first(3, 1)
     own[...] = jnp.zeros(own.shape, F32)
 
     @pl.when(straight)
     def _():
-        fwd(1, (0, 1))
+        fwd(1, (0, 1), (False,))
         to_x(0)
         fwd(1, (2, 3))
         to_x(1)
         to_x(2)
-        fwd(2, (0,))
         to_x(3)
-        fwd(2, (1,))
+        fwd(2, (0, 1))
         here(0)
         from_x(0)
         fwd(2, (2,))
@@ -344,34 +353,63 @@
         fwd(1, (3,))
         here(0)
         from_x(0)
-        fwd(2, (0,))
         here(1)
         from_x(1)
-        fwd(2, (1,))
-
+
+    even = lax.rem(z, 2) == 0
+    edge = (z == 0) | (z == nz - 1)
+
+    @pl.when(crossed & jnp.logical_not(edge))
+    def _():
+        fwd(2, (0, 1))
+
+    from_x(2)
+    from_x(3)
     here(2)
-    from_x(2)
+
+    @pl.when(crossed & jnp.logical_not(edge))
+    def _():
+        fwd(2, (2, 3))
+
     here(3)
-    from_x(3)
-
-    @pl.when(crossed)
-    def _():
-        fwd(2, (2, 3))
-
-    ready()
-    consume(z // 2 * 2, 2)
+
+    for other in (1, 0):
+        ready(other)
+        v = 1 - x if other else x
+
+        @pl.when(even & (z > 0))
+        def _():
+            consume(z - 2, 2, v)
+
+        consume(z // 2 * 2, 2, v)
+
+        @pl.when(jnp.logical_not(even) & (z < nz - 1))
+        def _():
+            consume(z + 1, 2, v)
+
+    @pl.when(crossed & edge)
+    def _():
+        fwd(2)
 
     def tail(t, carry):
-        for near, far in ((2 * (z // 2 - t) + 1, 2 * (z // 2 - t)), (2 * (z // 2 + t), 2 * (z // 2 + t) + 1)):
-            @pl.when((near >= 0) & (near < nz))
-            def _():
-                consume(near, 1)
+        base = z // 2 * 2
+        inner = base + jnp.where(even, -2 * t, 2 * t)
+        near = jnp.where(even, base + 2 * t, base - 2 * t + 1)
+        far = jnp.where(even, near + 1, near - 1)
+
+        @pl.when((t > 1) & (inner >= 0) & (inner < nz))
+        def _():
+            consume(inner, 2)
+
+        @pl.when((near >= 0) & (near < nz))
+        def _():
+            consume(near, 1)
 
         fwd(2 * t + 1)
-        for near, far in ((2 * (z // 2 - t) + 1, 2 * (z // 2 - t)), (2 * (z // 2 + t), 2 * (z // 2 + t) + 1)):
-            @pl.when((near >= 0) & (near < nz))
-            def _():
-                consume(far, 1)
+
+        @pl.when((near >= 0) & (near < nz))
+        def _():
+            consume(far, 1)
 
         @pl.when(2 * t + 2 < nz)
         def _():

time: 24.9 us -> 24.6 us (0.988)
  Pallas kernels: 24.1 us -> 23.8 us
    pallas_call x1, Pallas kernels: 24.1 us -> 23.8 us  [step(): pl.pallas_call(functools.partial(kernel, nb, ng), out_shape=pltpu.VMEM((2...]
where the time goes in v4:
time: 24.6 us; the launch traced here: 24.4 us
  Pallas kernels  23.8 us (97%)
  local copies, waits for them, and re-layouts  0.68 us (3%)
    pallas_call x1, Pallas kernels, step(): pl.pallas_call(functools.partial(kernel, nb, ng), out_shape=pltpu.VMEM((2...  23.8 us
    unnamed x1, local copies, waits for them, and re-layouts  0.68 us

profile of v4, /device:TPU:5, one launch (start us, length us, event | category | flops | bytes accessed | tf_op | source)
XLA Modules:
  0.0 24.4 jit_solution(6499342524005037087)
XLA Ops:
  0.0 23.8 %shard_map.64 = f32[2,96,192]{2,1,0:T(8,128)S(1)} custom-call(bf16[2,96,512]{2,1,0:T(8,128)(2,1)} %el.1, bf16[2,2,512,2048]{3,2,1,0:T(8,128)(2,1)} %wh.1, f32[768]{0:T(1024)} %en_h.1, s32[768]{0:T(1024)} %bos_h.1, f32[2]{0:T(128)} %fp_h.1, f32[2]{0:T(128)} %fw_h.1), custom_call_target="tpu_custom_call" | custom-call | tf_op jit(solution)/shard_map/pallas_call | solution.py:486
  23.8 0.7 %copy.8 = f32[2,96,192]{2,1,0:T(8,128)} copy(f32[2,96,192]{2,1,0:T(8,128)S(1)} %shard_map.64) | data formatting | bytes 294912

commit v5 on v4

--- a/solution.py
+++ b/solution.py
@@ -118,7 +118,7 @@
     pl.semaphore_wait(barrier, ng + 1 + below + above)
 
     unit = rows // 6
-    pieces = ((0, 2 * unit), (2 * unit, 2 * unit), (4 * unit, unit), (5 * unit, unit))
+    pieces = ((0, unit), (unit, 2 * unit), (3 * unit, 2 * unit), (5 * unit, unit))
     parts = range(len(pieces))
 
     def block(zs, i):

time: 24.6 us -> 24.6 us (level)
  no operation moved by 1% of the time
where the time goes in v5:
time: 24.6 us; the launch traced here: 24.5 us
  Pallas kernels  23.8 us (97%)
  local copies, waits for them, and re-layouts  0.68 us (3%)
    pallas_call x1, Pallas kernels, step(): pl.pallas_call(functools.partial(kernel, nb, ng), out_shape=pltpu.VMEM((2...  23.8 us
    unnamed x1, local copies, waits for them, and re-layouts  0.68 us

profile of v5, /device:TPU:5, one launch (start us, length us, event | category | flops | bytes accessed | tf_op | source)
XLA Modules:
  0.0 24.5 jit_solution(18235939304107465192)
XLA Ops:
  0.0 23.8 %shard_map.64 = f32[2,96,192]{2,1,0:T(8,128)S(1)} custom-call(bf16[2,96,512]{2,1,0:T(8,128)(2,1)} %el.1, bf16[2,2,512,2048]{3,2,1,0:T(8,128)(2,1)} %wh.1, f32[768]{0:T(1024)} %en_h.1, s32[768]{0:T(1024)} %bos_h.1, f32[2]{0:T(128)} %fp_h.1, f32[2]{0:T(128)} %fw_h.1), custom_call_target="tpu_custom_call" | custom-call | tf_op jit(solution)/shard_map/pallas_call | solution.py:486
  23.8 0.7 %copy.8 = f32[2,96,192]{2,1,0:T(8,128)} copy(f32[2,96,192]{2,1,0:T(8,128)S(1)} %shard_map.64) | data formatting | bytes 294912

commit v6 on v4

--- a/solution.py
+++ b/solution.py
@@ -373,10 +373,21 @@
 
     here(3)
 
+    beside = jnp.where(z == 0, 2, nz - 3)
+    first_beside = edge & ((beside * NX + c) // per // 2 != y)
+
+    @pl.when(crossed & first_beside)
+    def _():
+        fwd(2)
+
     for other in (1, 0):
         ready(other)
         v = 1 - x if other else x
 
+        @pl.when(first_beside)
+        def _():
+            consume(beside, 1, v)
+
         @pl.when(even & (z > 0))
         def _():
             consume(z - 2, 2, v)
@@ -387,7 +398,7 @@
         def _():
             consume(z + 1, 2, v)
 
-    @pl.when(crossed & edge)
+    @pl.when(crossed & edge & jnp.logical_not(first_beside))
     def _():
         fwd(2)
 
@@ -401,7 +412,7 @@
         def _():
             consume(inner, 2)
 
-        @pl.when((near >= 0) & (near < nz))
+        @pl.when((near >= 0) & (near < nz) & ((t > 1) | jnp.logical_not(first_beside)))
         def _():
             consume(near, 1)
 

time: 24.6 us -> 24.6 us (level)
  no operation moved by 1% of the time
where the time goes in v6:
time: 24.6 us; the launch traced here: 24.4 us
  Pallas kernels  23.8 us (97%)
  local copies, waits for them, and re-layouts  0.68 us (3%)
    pallas_call x1, Pallas kernels, step(): pl.pallas_call(functools.partial(kernel, nb, ng), out_shape=pltpu.VMEM((2...  23.8 us
    unnamed x1, local copies, waits for them, and re-layouts  0.68 us

profile of v6, /device:TPU:5, one launch (start us, length us, event | category | flops | bytes accessed | tf_op | source)
XLA Modules:
  0.0 24.4 jit_solution(10202885330375494566)
XLA Ops:
  0.0 23.8 %shard_map.64 = f32[2,96,192]{2,1,0:T(8,128)S(1)} custom-call(bf16[2,96,512]{2,1,0:T(8,128)(2,1)} %el.1, bf16[2,2,512,2048]{3,2,1,0:T(8,128)(2,1)} %wh.1, f32[768]{0:T(1024)} %en_h.1, s32[768]{0:T(1024)} %bos_h.1, f32[2]{0:T(128)} %fp_h.1, f32[2]{0:T(128)} %fw_h.1), custom_call_target="tpu_custom_call" | custom-call | tf_op jit(solution)/shard_map/pallas_call | solution.py:497
  23.8 0.7 %copy.8 = f32[2,96,192]{2,1,0:T(8,128)} copy(f32[2,96,192]{2,1,0:T(8,128)S(1)} %shard_map.64) | data formatting | bytes 294912
